TPU v7x, 32 devices: a whole 2x2x4 slice. The times are simulated.
32 devices in a mesh: ea: 4 (over y, x), row: 4 (over z), col: 2 (over core).
Axes of the slice: x: 2, y: 2, z: 4, core: 2. Of those that a mesh axis runs over, the one named last changes fastest.
Arguments:
- weights: float32 [4, 256, 2048], P('ea', 'row', 'col'), parts along dimension 0, may hold values from -6 to 6
- codebook: float32 [4, 16, 2, 256], P('ea', 'col'), parts along dimension 0, may hold values from -4 to 4
- assign: int32 [4, 256, 1024], P('ea', 'row', 'col'), parts along dimension 0, may hold values from 0 to 255
- chol_upper: float32 [4, 2048, 2048], P('ea', 'row', 'col'), parts along dimension 0, may hold values from 0 to 1.4, as said below
- inv_blocks: float32 [4, 16, 128, 128], P('ea', 'col'), parts along dimension 0, may hold values from -1 to 1.5, as said below
Outputs:
- errors: float32 [4, 256, 2048], P('ea', 'row', 'col'), parts along dimension 0
- row_loss: float32 [4, 256], P('ea', 'row'), parts along dimension 0
- codeword_mass: float32 [4, 16, 256], P('ea', 'col'), parts along dimension 0
There are 4 independent parts, one for each index of `ea`. A program takes and returns all parts, laid end to end along the dimension named above; each array names one. Nothing has to cross between parts.
Inputs may be any that keep to these rules, and one draw needn't show every extreme that they name: `chol_upper`: upper triangular with a positive diagonal. inv_blocks[x, b] is the inverse of the diagonal block of chol_upper[x] on rows and columns [b * 128, (b + 1) * 128).
All inputs are finite; a program needn't handle non-finite values.
Results may differ from a plain program's by a relative error of at most 0.0001.
Values sent between devices are 32-bit elements; how exact they have to be, the bound alone decides.
A program may use at most 64 MiB of HBM per device.

v0:
```python
import jax
import jax.numpy as jnp
from jax import lax
from jax.sharding import PartitionSpec as P


def from_root(value, axis, source):
    kept = jnp.where(lax.axis_index(axis) == source, value, 0).astype(value.dtype)
    return lax.psum(kept, axis)


def flat_labels(assign, half_block, code_count):
    pair_count = assign.shape[2]
    offsets = jnp.arange(pair_count, dtype=jnp.int32) // half_block * code_count
    return assign + offsets[None, None, :]


def lookup_local(codebook, labels):
    experts, row_count, pair_count = labels.shape
    code_table = jnp.transpose(codebook, (0, 2, 1, 3)).reshape(experts, 2, -1)

    def select(rows_table, indices):
        return jnp.stack(
            [jnp.take(rows_table[0], indices), jnp.take(rows_table[1], indices)], axis=-1
        )

    picked = jax.vmap(select)(code_table, labels)
    return picked.reshape(experts, row_count, 2 * pair_count)


def mass_by_code(errors, labels, local_blocks, code_count):
    experts, row_count, width = errors.shape
    squared = errors * errors
    paired = squared.reshape(experts, row_count, width // 2, 2).sum(axis=3)

    def summed(values, marks):
        return jax.ops.segment_sum(
            values.reshape(-1), marks.reshape(-1), num_segments=local_blocks * code_count
        )

    return jax.vmap(summed)(paired, labels).reshape(experts, local_blocks, code_count)


def local(weights, codebook, assign, chol_upper, inv_blocks):
    block_size = inv_blocks.shape[2]
    local_blocks = inv_blocks.shape[1]
    local_width = weights.shape[2]
    code_count = codebook.shape[3]
    column_rank = lax.axis_index("col")
    block_total = local_blocks * lax.axis_size("col")
    labels = flat_labels(assign, block_size // 2, code_count)
    quantized = lookup_local(codebook, labels)
    column_ids = column_rank * local_width + jnp.arange(local_width, dtype=jnp.int32)
    stacked = lax.all_gather(chol_upper, "row", axis=1, tiled=True)

    def panel_of(number):
        return lax.dynamic_slice_in_dim(stacked, number * block_size, block_size, 1)

    def own_block(current, number):
        return lax.dynamic_slice_in_dim(current, number % local_blocks * block_size, block_size, 2)

    def block_error(current_block, number):
        owner_rank = number // local_blocks
        inverse = lax.dynamic_index_in_dim(inv_blocks, number % local_blocks, 1, keepdims=False)
        target = own_block(quantized, number)

        def compute():
            return jnp.einsum(
                "xrc,xcd->xrd", current_block - target, inverse, precision=lax.Precision.HIGHEST
            )

        def nothing():
            return jnp.zeros(current_block.shape, jnp.float32)

        computed = lax.cond(owner_rank == column_rank, compute, nothing)
        return from_root(computed, "col", owner_rank)

    def propagate(current, error_block, panel_rows, number, targets):
        beyond = targets >= (number + 1) * block_size
        masked = jnp.where(beyond[None, None, :], panel_rows, 0.0)
        return current - jnp.einsum(
            "xrc,xcd->xrd", error_block, masked, precision=lax.Precision.HIGHEST
        )

    def record(errors, error_block, number):
        owner_rank = number // local_blocks
        offset = number % local_blocks * block_size
        previous = lax.dynamic_slice_in_dim(errors, offset, block_size, 2)
        chosen = jnp.where(owner_rank == column_rank, error_block, previous)
        return lax.dynamic_update_slice_in_dim(errors, chosen, offset, 2)

    blank = jnp.zeros(weights.shape, jnp.float32)

    def advance(number, state_pair):
        current, errors = state_pair
        error_block = block_error(own_block(current, number), number)
        errors = record(errors, error_block, number)
        current = propagate(current, error_block, panel_of(number), number, column_ids)
        return (current, errors)

    current, errors = lax.fori_loop(0, block_total, advance, (weights, blank))
    row_loss = lax.psum(jnp.sum(errors * errors, axis=2), "col")
    local_mass = mass_by_code(errors, labels, local_blocks, code_count)
    codeword_mass = lax.psum(local_mass, "row")
    return (errors, row_loss, codeword_mass)


def solution(mesh):
    return jax.shard_map(
        local,
        mesh=mesh,
        in_specs=(
            P("ea", "row", "col"),
            P("ea", "col", None, None),
            P("ea", "row", "col"),
            P("ea", "row", "col"),
            P("ea", "col", None, None),
        ),
        out_specs=(P("ea", "row", "col"), P("ea", "row"), P("ea", "col", None)),
        check_vma=False,
    )
```

profile of v0, /device:TPU:0, one launch (start us, length us, event | category | flops | bytes accessed | tf_op | source)
XLA Modules:
  0.0 742.4 jit_solution(10534728693327028452)
XLA Ops:
  9.9 190.2 %gather_fusion.1 = f32[32768]{0:T(1024)S(1)} fusion(f32[1,2048]{1,0:T(1,128)S(1)} %get-tuple-element.332, s32[32768]{0:T(1024)S(1)} %bitcast.50), kind=kCustom, calls=%fused_computation.1.clone | custom fusion | bytes 524288 | tf_op jit(solution)/shard_map/vmap(jit(_take))/gather | solution.py:24
  200.2 190.2 %gather_fusion = f32[32768]{0:T(1024)S(1)} fusion(f32[1,2048]{1,0:T(1,128)S(1)} %get-tuple-element.333, s32[32768]{0:T(1024)S(1)} %bitcast.51), kind=kCustom, calls=%fused_computation.clone | custom fusion | bytes 524288 | tf_op jit(solution)/shard_map/vmap(jit(_take))/gather | solution.py:24
  392.2 98.7 %while.18 = (s32[]{:T(128)}, f32[1,64,1024]{2,1,0:T(8,128)S(1)}, f32[1,64,1024]{2,1,0:T(8,128)S(1)}, s32[]{:T(128)}, f32[1,64,1024]{2,1,0:T(8,128)S(1)}, /*index...) while((s32[]{:T(128)}, f32[1,64,1024]{2,1,0:T(8,128)S(1)}, ...), condition=%wide.region_4.6_spmd.clone, body=%wide.region_0.5_spmd.clone.sunk | while | flops 113477664 | bytes 1477659 | solution.py:101
  393.4 3.4 psum.32
  399.6 3.4 psum.32
  403.0 1.5 fusion.35
  405.7 3.4 psum.32
  411.9 3.4 psum.32
  418.0 3.4 psum.32
  424.2 3.4 psum.32
  427.6 1.5 fusion.35
  430.3 3.4 psum.32
  436.5 3.4 psum.32
  441.6 4.6 psum.32
  447.9 4.5 psum.32
  454.1 4.5 psum.32
  460.2 4.5 psum.32
  466.4 4.5 psum.32
  472.5 4.5 psum.32
  478.7 4.5 psum.32
  484.8 4.5 psum.32
  491.0 3.0 psum.28
  495.0 226.3 %scatter_custom_fusion = f32[2048]{0:T(1024)S(1)} fusion(s32[32768]{0:T(1024)S(1)} %broadcast_select_fusion.1, f32[32768]{0:T(1024)S(1)} %bitcast.55, f32[]{:T(128)} %constant.181.clone.1), kind=kCustom, calls=%fused_computation.45 | custom fusion | flops 32768 | bytes 8196
  721.4 14.2 %psum.29 = f32[1,8,256]{2,1,0:T(8,128)} all-reduce(f32[1,8,256]{2,1,0:T(8,128)S(1)} %reshape.106), channel_id=1, replica_groups=mesh['ea'=4,'row'=4,'col'=2] {'row'}, use_global_device_ids=true, to_apply=%region_9.11 | all-reduce | flops 2048 | bytes 16384 | tf_op jit(solution)/shard_map/psum | solution.py:104
  (129 shorter events, 45.1 us)
Async XLA Ops:
  7.2 385.0 %all-gather.2.cloned.1.call-start = ((), (), s32[]{:S(2)}) async-start(), calls=%async_computation | async-start | bytes 10485760 | tf_op jit(solution)/shard_map/all_gather | solution.py:54
  200.2 190.9 %copy-start.3 = (s32[2]{0:T(128)S(1)}, s32[2]{0:T(128)}, u32[]{:S(2)}) copy-start(s32[2]{0:T(128)} %constant.194) | copy-start | bytes 28
  200.2 191.3 %copy-start.2 = (s32[2]{0:T(128)S(1)}, s32[2]{0:T(128)}, u32[]{:S(2)}) copy-start(s32[2]{0:T(128)} %constant.197) | copy-start | bytes 28
  200.2 192.0 %copy-start = (f32[1,64,1024]{2,1,0:T(8,128)S(1)}, f32[1,64,1024]{2,1,0:T(8,128)}, u32[]{:S(2)}) copy-start(f32[1,64,1024]{2,1,0:T(8,128)} %param.11) | copy-start | bytes 786436
  490.9 244.6 %copy-start.1 = (f32[1,64,1024]{2,1,0:T(8,128)}, f32[1,64,1024]{2,1,0:T(8,128)S(1)}, u32[]{:S(2)}) copy-start(f32[1,64,1024]{2,1,0:T(8,128)S(1)} %get-tuple-element.263) | copy-start | bytes 786436
Sparse Core Ops, SparseCore 0:
  9.5 152.3 all-gather.1
where the time goes:
time: 744 us; the launch traced here: 742 us
  local copies, waits for them, and re-layouts  382 us (51%)
  other arithmetic  230 us (31%)
  blocking collectives  80.4 us (11%)
  matrix products  33.1 us (4%)
  between operations  14.3 us (2%)
    unnamed x5, other arithmetic  227 us
    gather x3, local copies, waits for them, and re-layouts, select(): jnp.take(rows_table[0], indices)  190 us
    gather x2, local copies, waits for them, and re-layouts, select(): jnp.take(rows_table[1], indices)  190 us
    psum x16, blocking collectives, from_root(): return lax.psum(kept, axis)  63.3 us
    dot_general x16, matrix products, propagate(): jnp.einsum('xrc,xcd->xrd', error_block, masked, precision=lax.Precision.H...  24.4 us
  transfers between devices with their start and end apart: 1, of which 0 were waited for; matrix products, arithmetic and copies ran while one was open for 52% of the time, Pallas kernels for 0%

commit v1 on v0

--- a/solution.py
+++ b/solution.py
@@ -2,11 +2,16 @@
 import jax.numpy as jnp
 from jax import lax
 from jax.sharding import PartitionSpec as P
+from jax.lax import all_gather
+
+
+def choose_case_all(payload, group_axis):
+    return all_gather(payload, group_axis).sum(axis=0)
 
 
 def from_root(value, axis, source):
     kept = jnp.where(lax.axis_index(axis) == source, value, 0).astype(value.dtype)
-    return lax.psum(kept, axis)
+    return choose_case_all(kept, axis)
 
 
 def flat_labels(assign, half_block, code_count):

time: 744 us -> 719 us (0.966)
  blocking collectives: 80.4 us -> 55.3 us
    psum x16 -> x0, blocking collectives: 63.3 us -> none  [from_root(): return lax.psum(kept, axis)]
    all_gather x0 -> x16, blocking collectives: none -> 38.1 us  [choose_case_all(): return all_gather(payload, group_axis).sum(axis=0)]
  transfers between devices with their start and end apart: 1 -> 1, of which waited for: 0 -> 0; matrix products, arithmetic and copies ran while one was open for 52% -> 54% of each run, Pallas kernels for 0% -> 0%
where the time goes in v1:
time: 719 us; the launch traced here: 717 us
  local copies, waits for them, and re-layouts  382 us (53%)
  other arithmetic  230 us (32%)
  blocking collectives  55.3 us (8%)
  matrix products  33 us (5%)
  between operations  14.3 us (2%)
    unnamed x5, other arithmetic  227 us
    gather x3, local copies, waits for them, and re-layouts, select(): jnp.take(rows_table[0], indices)  190 us
    gather x2, local copies, waits for them, and re-layouts, select(): jnp.take(rows_table[1], indices)  190 us
    all_gather x16, blocking collectives, choose_case_all(): return all_gather(payload, group_axis).sum(axis=0)  38.1 us
    dot_general x16, matrix products, propagate(): jnp.einsum('xrc,xcd->xrd', error_block, masked, precision=lax.Precision.H...  24.3 us
  transfers between devices with their start and end apart: 1, of which 0 were waited for; matrix products, arithmetic and copies ran while one was open for 54% of the time, Pallas kernels for 0%

profile of v1, /device:TPU:0, one launch (start us, length us, event | category | flops | bytes accessed | tf_op | source)
XLA Modules:
  0.0 717.2 jit_solution(10817993993569206558)
XLA Ops:
  9.9 190.2 %gather_fusion.1 = f32[32768]{0:T(1024)S(1)} fusion(f32[1,2048]{1,0:T(1,128)S(1)} %get-tuple-element.332, s32[32768]{0:T(1024)S(1)} %bitcast.54), kind=kCustom, calls=%fused_computation.1.clone | custom fusion | bytes 524288 | tf_op jit(solution)/shard_map/vmap(jit(_take))/gather | solution.py:29
  200.2 190.2 %gather_fusion = f32[32768]{0:T(1024)S(1)} fusion(f32[1,2048]{1,0:T(1,128)S(1)} %get-tuple-element.333, s32[32768]{0:T(1024)S(1)} %bitcast.55), kind=kCustom, calls=%fused_computation.clone | custom fusion | bytes 524288 | tf_op jit(solution)/shard_map/vmap(jit(_take))/gather | solution.py:29
  392.2 73.4 %while.18 = (s32[]{:T(128)}, f32[1,64,1024]{2,1,0:T(8,128)S(1)}, f32[1,64,1024]{2,1,0:T(8,128)S(1)}, s32[]{:T(128)}, f32[1,64,1024]{2,1,0:T(8,128)S(1)}, /*index...) while((s32[]{:T(128)}, f32[1,64,1024]{2,1,0:T(8,128)S(1)}, ...), condition=%wide.region_4.6_spmd.clone, body=%wide.region_0.5_spmd.clone.sunk | while | flops 113477664 | bytes 1608743 | solution.py:106
  393.4 1.9 all-gather.3
  395.3 1.5 fusion.37
  398.0 1.9 all-gather.3
  402.6 1.9 all-gather.3
  407.2 1.9 all-gather.3
  411.8 1.9 all-gather.3
  416.4 1.9 all-gather.3
  418.3 1.5 fusion.37
  421.0 1.9 all-gather.3
  425.6 1.9 all-gather.3
  429.1 2.7 all-gather.3
  433.5 2.9 all-gather.3
  438.1 2.9 all-gather.3
  442.7 2.9 all-gather.3
  447.3 2.9 all-gather.3
  451.9 2.9 all-gather.3
  456.6 2.9 all-gather.3
  461.2 2.9 all-gather.3
  465.8 3.0 psum.14
  469.8 226.3 %scatter_custom_fusion = f32[2048]{0:T(1024)S(1)} fusion(s32[32768]{0:T(1024)S(1)} %broadcast_select_fusion.1, f32[32768]{0:T(1024)S(1)} %bitcast.59, f32[]{:T(128)} %constant.181.clone.1), kind=kCustom, calls=%fused_computation.45 | custom fusion | flops 32768 | bytes 8196
  696.1 14.2 %psum.15 = f32[1,8,256]{2,1,0:T(8,128)} all-reduce(f32[1,8,256]{2,1,0:T(8,128)S(1)} %reshape.106), channel_id=1, replica_groups=mesh['ea'=4,'row'=4,'col'=2] {'row'}, use_global_device_ids=true, to_apply=%region_9.11 | all-reduce | flops 2048 | bytes 16384 | tf_op jit(solution)/shard_map/psum | solution.py:109
  (145 shorter events, 45.1 us)
Async XLA Ops:
  7.2 385.0 %all-gather.6.cloned.1.call-start = ((), (), s32[]{:S(2)}) async-start(), calls=%async_computation | async-start | bytes 10485760 | tf_op jit(solution)/shard_map/all_gather | solution.py:59
  200.2 190.9 %copy-start.3 = (s32[2]{0:T(128)S(1)}, s32[2]{0:T(128)}, u32[]{:S(2)}) copy-start(s32[2]{0:T(128)} %constant.194) | copy-start | bytes 28
  200.2 191.3 %copy-start.2 = (s32[2]{0:T(128)S(1)}, s32[2]{0:T(128)}, u32[]{:S(2)}) copy-start(s32[2]{0:T(128)} %constant.197) | copy-start | bytes 28
  200.2 192.0 %copy-start = (f32[1,64,1024]{2,1,0:T(8,128)S(1)}, f32[1,64,1024]{2,1,0:T(8,128)}, u32[]{:S(2)}) copy-start(f32[1,64,1024]{2,1,0:T(8,128)} %param.11) | copy-start | bytes 786436
  465.7 244.7 %copy-start.1 = (f32[1,64,1024]{2,1,0:T(8,128)}, f32[1,64,1024]{2,1,0:T(8,128)S(1)}, u32[]{:S(2)}) copy-start(f32[1,64,1024]{2,1,0:T(8,128)S(1)} %get-tuple-element.263) | copy-start | bytes 786436
Sparse Core Ops, SparseCore 0:
  9.5 152.3 all-gather.5
